TPU v7x, 32 devices: a whole 2x2x4 slice. The times are simulated.
32 devices in a mesh: col: 16 (over z, x, core), row: 2 (over y).
Axes of the slice: x: 2, y: 2, z: 4, core: 2. Of those that a mesh axis runs over, the one named last changes fastest.
Arguments:
- blocks: float32 [16, 2, 24, 128, 128], P('col', 'row'), may hold values from -0.21875 to 0.21875
- row_index: int32 [16, 2, 24], P('col', 'row'), may hold values from 0 to 63
- col_index: int32 [16, 2, 24], P('col', 'row'), may hold values from 0 to 23
- counts: int32 [16, 2], P('col', 'row'), may hold values from 12 to 24, as said below
- rhs: float32 [16384], P(('row', 'col')), may hold values from -6 to 6
- lower: float32 [49152], P(('col', 'row')), may hold values from -0.6 to -0.05
- upper: float32 [49152], P(('col', 'row')), may hold values from 0.05 to 0.6
- primal_start: float32 [49152], P(('col', 'row')), may hold values from -0.05 to 0.05
- dual_start: float32 [16384], P(('row', 'col')), may hold values from -4 to 4
Outputs:
- primal: float32 [49152], P(('col', 'row'))
- dual: float32 [16384], P(('row', 'col'))
- norms: float32 [3, 2], replicated
Inputs may be any that keep to these rules, and one draw needn't show every extreme that they name: `counts`: each list has between 12 and 24 live slots; both ends are reached in every draw.
All inputs are finite; a program needn't handle non-finite values.
Results may differ from a plain program's by a relative error of at most 0.0001.
Values sent between devices are 32-bit elements; how exact they have to be, the bound alone decides.
A program may use at most 64 MiB of HBM per device.

v0:
```python
import jax
import jax.numpy as jnp
from jax import lax
from jax.sharding import PartitionSpec as P

ITERS = 3


def local(blocks, row_index, col_index, counts, rhs, lower, upper, primal_start, dual_start):
    slot_count = blocks.shape[2]
    side = blocks.shape[3]
    tiles = blocks.reshape(slot_count, side, side)
    rows = row_index.reshape(slot_count)
    cols = col_index.reshape(slot_count)
    live = (jnp.arange(slot_count, dtype=jnp.int32) < counts.reshape(())).astype(jnp.float32)
    n_col = lax.axis_size("col")
    n_row = lax.axis_size("row")
    primal_len = primal_start.shape[0]
    dual_len = dual_start.shape[0]
    col_blocks = primal_len * n_row // side
    row_blocks = dual_len * n_col // side
    tau = 0.4
    sigma = 0.4
    records = []

    def record(resid_sq, moved_sq):
        total_resid, total_moved = lax.psum((resid_sq, moved_sq), ("col", "row"))
        records.append(jnp.stack([jnp.sqrt(total_resid), jnp.sqrt(total_moved)]))

    primal_group, lower_group, upper_group = (
        lax.all_gather(primal_start, "row", axis=0, tiled=True),
        lax.all_gather(lower, "row", axis=0, tiled=True),
        lax.all_gather(upper, "row", axis=0, tiled=True),
    )
    dual_group, rhs_group = (
        lax.all_gather(dual_start, "col", axis=0, tiled=True),
        lax.all_gather(rhs, "col", axis=0, tiled=True),
    )
    primal_offset = lax.axis_index("row") * primal_len
    dual_offset = lax.axis_index("col") * dual_len
    for step in range(ITERS):
        pieces = dual_group.reshape(-1, side)[rows]
        prod = (
            jnp.einsum("kij,ki->kj", tiles, pieces, precision=lax.Precision.HIGHEST) * live[:, None]
        )
        grad = lax.psum(jax.ops.segment_sum(prod, cols, num_segments=col_blocks).reshape(-1), "row")
        primal_new = jnp.minimum(jnp.maximum(primal_group + tau * grad, lower_group), upper_group)
        extra = 2.0 * primal_new - primal_group
        apply_pieces = extra.reshape(-1, side)[cols]
        apply_prod = (
            jnp.einsum("kij,kj->ki", tiles, apply_pieces, precision=lax.Precision.HIGHEST)
            * live[:, None]
        )
        product = lax.psum(
            jax.ops.segment_sum(apply_prod, rows, num_segments=row_blocks).reshape(-1), "col"
        )
        resid = rhs_group - product
        dual_group = dual_group + sigma * resid
        moved_own = lax.dynamic_slice_in_dim(primal_new - primal_group, primal_offset, primal_len)
        resid_own = lax.dynamic_slice_in_dim(resid, dual_offset, dual_len)
        record(jnp.sum(resid_own * resid_own), jnp.sum(moved_own * moved_own))
        primal_group = primal_new
    primal_out = lax.dynamic_slice_in_dim(primal_group, primal_offset, primal_len)
    dual_out = lax.dynamic_slice_in_dim(dual_group, dual_offset, dual_len)
    norms = jnp.stack(records)
    return (primal_out, dual_out, norms)


def solution(mesh):
    in_specs = (
        P("col", "row", None, None, None),
        P("col", "row", None),
        P("col", "row", None),
        P("col", "row"),
        P(("row", "col")),
        P(("col", "row")),
        P(("col", "row")),
        P(("col", "row")),
        P(("row", "col")),
    )
    out_specs = (P(("col", "row")), P(("row", "col")), P())
    return jax.shard_map(local, mesh=mesh, in_specs=in_specs, out_specs=out_specs, check_vma=False)
```

profile of v0, /device:TPU:12, one launch (start us, length us, event | category | flops | bytes accessed | tf_op | source)
XLA Modules:
  0.0 322.5 jit_solution(8826910674664493860)
XLA Ops:
  0.7 0.8 reshape.230
  1.5 4.4 %all-gather = f32[2,1,1536]{2,1,0:T(1,128)S(1)} all-gather(f32[1,1,1536]{2,1,0:T(1,128)S(1)} %reshape.230), channel_id=1, replica_groups=mesh['col'=16,'row'=2] {'row'}, dimensions={0}, use_global_device_ids=true | all-gather | bytes 18432 | tf_op jit(solution)/shard_map/all_gather | solution.py:31
  5.9 0.7 reshape.236
  6.6 4.4 %all-gather.3 = f32[2,1,1536]{2,1,0:T(1,128)S(1)} all-gather(f32[1,1,1536]{2,1,0:T(1,128)S(1)} %reshape.236), channel_id=1, replica_groups=mesh['col'=16,'row'=2] {'row'}, dimensions={0}, use_global_device_ids=true | all-gather | bytes 18432 | tf_op jit(solution)/shard_map/all_gather | solution.py:33
  10.9 0.7 reshape.234
  11.6 4.4 %all-gather.2 = f32[2,1,1536]{2,1,0:T(1,128)S(1)} all-gather(f32[1,1,1536]{2,1,0:T(1,128)S(1)} %reshape.234), channel_id=1, replica_groups=mesh['col'=16,'row'=2] {'row'}, dimensions={0}, use_global_device_ids=true | all-gather | bytes 18432 | tf_op jit(solution)/shard_map/all_gather | solution.py:32
  16.0 19.1 %all-gather.1 = f32[16,1,512]{2,1,0:T(1,128)S(1)} all-gather(f32[1,1,512]{2,1,0:T(1,128)} %bitcast.129), channel_id=1, replica_groups=mesh['col'=16,'row'=2] {'col'}, dimensions={0}, use_global_device_ids=true | all-gather | bytes 34816 | tf_op jit(solution)/shard_map/all_gather | solution.py:36
  35.1 0.7 fusion.39
  36.4 1.4 fusion.10
  38.4 0.7 scatter_custom_fusion
  39.2 7.1 %psum.84 = f32[3072]{0:T(1024)S(1)} all-reduce(f32[3072]{0:T(1024)S(1)} %bitcast.126), channel_id=1, replica_groups=mesh['col'=16,'row'=2] {'row'}, use_global_device_ids=true, to_apply=%region_1.0 | all-reduce | flops 3072 | bytes 24576 | tf_op jit(solution)/shard_map/psum | solution.py:46
  46.3 17.2 %all-gather.4 = f32[16,1,512]{2,1,0:T(1,128)S(1)} all-gather(f32[1,1,512]{2,1,0:T(1,128)S(1)} %bitcast.130), channel_id=1, replica_groups=mesh['col'=16,'row'=2] {'col'}, dimensions={0}, use_global_device_ids=true | all-gather | bytes 34816 | tf_op jit(solution)/shard_map/all_gather | solution.py:37
  64.1 2.5 fusion.8
  66.6 0.9 scatter_custom_fusion.1
  67.5 54.3 %psum.85 = f32[8192]{0:T(1024)S(1)} all-reduce(f32[8192]{0:T(1024)S(1)} %bitcast.110), channel_id=1, replica_groups=mesh['col'=16,'row'=2] {'col'}, use_global_device_ids=true, to_apply=%region_3.0 | all-reduce | flops 8192 | bytes 65536 | tf_op jit(solution)/shard_map/psum | solution.py:54
  122.4 1.4 fusion.6
  123.8 0.7 scatter_custom_fusion.2
  124.5 8.1 %psum.86 = f32[3072]{0:T(1024)S(1)} all-reduce(f32[3072]{0:T(1024)S(1)} %bitcast.127), channel_id=1, replica_groups=mesh['col'=16,'row'=2] {'row'}, use_global_device_ids=true, to_apply=%region_5.0 | all-reduce | flops 3072 | bytes 24576 | tf_op jit(solution)/shard_map/psum | solution.py:46
  133.2 2.5 fusion.4
  135.8 0.9 scatter_custom_fusion.3
  136.7 57.6 %psum.87 = f32[8192]{0:T(1024)S(1)} all-reduce(f32[8192]{0:T(1024)S(1)} %bitcast.111), channel_id=1, replica_groups=mesh['col'=16,'row'=2] {'col'}, use_global_device_ids=true, to_apply=%region_7.0 | all-reduce | flops 8192 | bytes 65536 | tf_op jit(solution)/shard_map/psum | solution.py:54
  194.9 1.4 fusion.2
  196.3 0.7 scatter_custom_fusion.4
  197.0 7.1 %psum.88 = f32[3072]{0:T(1024)S(1)} all-reduce(f32[3072]{0:T(1024)S(1)} %bitcast.128), channel_id=1, replica_groups=mesh['col'=16,'row'=2] {'row'}, use_global_device_ids=true, to_apply=%region_9.0 | all-reduce | flops 3072 | bytes 24576 | tf_op jit(solution)/shard_map/psum | solution.py:46
  204.1 1.3 fusion.29
  206.1 2.5 fusion
  208.6 0.9 scatter_custom_fusion.5
  209.5 57.6 %psum.89 = f32[8192]{0:T(1024)S(1)} all-reduce(f32[8192]{0:T(1024)S(1)} %bitcast.109), channel_id=1, replica_groups=mesh['col'=16,'row'=2] {'col'}, use_global_device_ids=true, to_apply=%region_11.0 | all-reduce | flops 8192 | bytes 65536 | tf_op jit(solution)/shard_map/psum | solution.py:54
  267.1 1.3 multiply_reduce_fusion.2
  268.4 0.7 multiply_reduce_fusion.4
  269.1 48.5 %all-reduce = (f32[]{:T(128)}, f32[]{:T(128)}, f32[]{:T(128)}, f32[]{:T(128)}, f32[]{:T(128)}, /*index=5*/f32[]{:T(128)}) all-reduce(f32[]{:T(128)} %get-tuple-element.11, f32[]{:T(128)} %get-tuple-element.29, f32[]{:T(128)} %get-tuple-element.10, f32[]{:T(128)} %get-tuple-element.31, ...), channel_id=1, replica_groups=mesh['col'=16,'row'=2] {'col','row'}, use_global_device_ids=true, to_apply=%region_23.0 | all-reduce | flops 6 | bytes 48 | tf_op jit(solution)/shard_map/psum | solution.py:27
  321.9 0.7 copy.13
  (26 shorter events, 3.7 us)
Async XLA Ops:
  0.6 35.7 %copy-start = (f32[1,1,24,128,128]{4,3,2,1,0:T(8,128)S(1)}, f32[1,1,24,128,128]{4,3,2,1,0:T(8,128)}, u32[]{:S(2)}) copy-start(f32[1,1,24,128,128]{4,3,2,1,0:T(8,128)} %param.9) | copy-start | bytes 4718596
  0.6 37.8 %copy-start.2 = (s32[1,1,24]{2,1,0:T(1,128)S(1)}, s32[1,1,24]{2,1,0:T(1,128)}, u32[]{:S(2)}) copy-start(s32[1,1,24]{2,1,0:T(1,128)} %param.11) | copy-start | bytes 292
  0.7 45.6 %copy-start.1 = (f32[512]{0:T(512)S(1)}, f32[512]{0:T(512)}, u32[]{:S(2)}) copy-start(f32[512]{0:T(512)} %param.13) | copy-start | bytes 6148
where the time goes:
time: 323 us
  blocking collectives  290 us (90%)
  matrix products  11.9 us (4%)
  other arithmetic  9.14 us (3%)
  local copies, waits for them, and re-layouts  6.29 us (2%)
  between operations  5.46 us (2%)
    psum x3, blocking collectives, local(): lax.psum(jax.ops.segment_sum(apply_prod, rows, num_segments=row_blocks).r...  170 us
    psum x1, blocking collectives, record(): total_resid, total_moved = lax.psum((resid_sq, moved_sq), ('col', 'row'))  48.5 us
    psum x3, blocking collectives, local(): lax.psum(jax.ops.segment_sum(prod, cols, num_segments=col_blocks).reshape...  22.3 us
    all_gather x1, blocking collectives, local(): lax.all_gather(dual_start, 'col', axis=0, tiled=True)  19.1 us
    all_gather x1, blocking collectives, local(): lax.all_gather(rhs, 'col', axis=0, tiled=True)  17.2 us
    dot_general x3, matrix products, local(): jnp.einsum('kij,kj->ki', tiles, apply_pieces, precision=lax.Precision.HIG...  7.62 us

commit v1 on v0

--- a/solution.py
+++ b/solution.py
@@ -43,7 +43,12 @@
         prod = (
             jnp.einsum("kij,ki->kj", tiles, pieces, precision=lax.Precision.HIGHEST) * live[:, None]
         )
-        grad = lax.psum(jax.ops.segment_sum(prod, cols, num_segments=col_blocks).reshape(-1), "row")
+        grad = jnp.sum(
+            lax.all_gather(
+                jax.ops.segment_sum(prod, cols, num_segments=col_blocks).reshape(-1), "row"
+            ),
+            axis=0,
+        )
         primal_new = jnp.minimum(jnp.maximum(primal_group + tau * grad, lower_group), upper_group)
         extra = 2.0 * primal_new - primal_group
         apply_pieces = extra.reshape(-1, side)[cols]

time: 323 us -> 313 us (0.969)
  blocking collectives: 290 us -> 280 us
    psum x3 -> x0, blocking collectives: 22.3 us -> none  [local(): lax.psum(jax.ops.segment_sum(prod, cols, num_segments=col_blocks).reshape...]
    all_gather x0 -> x3, blocking collectives: none -> 13.2 us  [local(): lax.all_gather(jax.ops.segment_sum(prod, cols, num_segments=col_blocks).r...]
where the time goes in v1:
time: 313 us
  blocking collectives  280 us (89%)
  matrix products  11.9 us (4%)
  other arithmetic  9.25 us (3%)
  local copies, waits for them, and re-layouts  6.29 us (2%)
  between operations  5.49 us (2%)
    psum x3, blocking collectives, local(): lax.psum(jax.ops.segment_sum(apply_prod, rows, num_segments=row_blocks).r...  170 us
    psum x1, blocking collectives, record(): total_resid, total_moved = lax.psum((resid_sq, moved_sq), ('col', 'row'))  47.5 us
    all_gather x1, blocking collectives, local(): lax.all_gather(dual_start, 'col', axis=0, tiled=True)  19.1 us
    all_gather x1, blocking collectives, local(): lax.all_gather(rhs, 'col', axis=0, tiled=True)  17.2 us
    all_gather x3, blocking collectives, local(): lax.all_gather(jax.ops.segment_sum(prod, cols, num_segments=col_blocks).r...  13.2 us
    dot_general x3, matrix products, local(): jnp.einsum('kij,kj->ki', tiles, apply_pieces, precision=lax.Precision.HIG...  7.62 us

profile of v1, /device:TPU:12, one launch (start us, length us, event | category | flops | bytes accessed | tf_op | source)
XLA Modules:
  0.0 312.6 jit_solution(9000711618814326744)
XLA Ops:
  0.7 0.8 reshape.218
  1.5 4.4 %all-gather = f32[2,1,1536]{2,1,0:T(1,128)S(1)} all-gather(f32[1,1,1536]{2,1,0:T(1,128)S(1)} %reshape.218), channel_id=1, replica_groups=mesh['col'=16,'row'=2] {'row'}, dimensions={0}, use_global_device_ids=true | all-gather | bytes 18432 | tf_op jit(solution)/shard_map/all_gather | solution.py:31
  5.9 0.7 reshape.226
  6.6 4.4 %all-gather.4 = f32[2,1,1536]{2,1,0:T(1,128)S(1)} all-gather(f32[1,1,1536]{2,1,0:T(1,128)S(1)} %reshape.226), channel_id=1, replica_groups=mesh['col'=16,'row'=2] {'row'}, dimensions={0}, use_global_device_ids=true | all-gather | bytes 18432 | tf_op jit(solution)/shard_map/all_gather | solution.py:33
  10.9 0.7 reshape.224
  11.6 4.4 %all-gather.3 = f32[2,1,1536]{2,1,0:T(1,128)S(1)} all-gather(f32[1,1,1536]{2,1,0:T(1,128)S(1)} %reshape.224), channel_id=1, replica_groups=mesh['col'=16,'row'=2] {'row'}, dimensions={0}, use_global_device_ids=true | all-gather | bytes 18432 | tf_op jit(solution)/shard_map/all_gather | solution.py:32
  16.0 19.1 %all-gather.1 = f32[16,1,512]{2,1,0:T(1,128)S(1)} all-gather(f32[1,1,512]{2,1,0:T(1,128)} %bitcast.129), channel_id=1, replica_groups=mesh['col'=16,'row'=2] {'col'}, dimensions={0}, use_global_device_ids=true | all-gather | bytes 34816 | tf_op jit(solution)/shard_map/all_gather | solution.py:36
  35.1 0.7 fusion.39
  36.4 1.4 fusion.10
  38.4 0.7 scatter_custom_fusion
  39.2 4.4 %all-gather.2 = f32[2,1,3072]{2,1,0:T(1,128)S(1)} all-gather(f32[1,1,3072]{2,1,0:T(1,128)S(1)} %bitcast.126), channel_id=1, replica_groups=mesh['col'=16,'row'=2] {'row'}, dimensions={0}, use_global_device_ids=true | all-gather | bytes 36864 | tf_op jit(solution)/shard_map/all_gather | solution.py:47
  43.6 17.2 %all-gather.5 = f32[16,1,512]{2,1,0:T(1,128)S(1)} all-gather(f32[1,1,512]{2,1,0:T(1,128)S(1)} %bitcast.130), channel_id=1, replica_groups=mesh['col'=16,'row'=2] {'col'}, dimensions={0}, use_global_device_ids=true | all-gather | bytes 34816 | tf_op jit(solution)/shard_map/all_gather | solution.py:37
  61.4 2.5 fusion.8
  64.0 0.9 scatter_custom_fusion.1
  64.9 54.3 %psum.63 = f32[8192]{0:T(1024)S(1)} all-reduce(f32[8192]{0:T(1024)S(1)} %bitcast.110), channel_id=1, replica_groups=mesh['col'=16,'row'=2] {'col'}, use_global_device_ids=true, to_apply=%region_3.0 | all-reduce | flops 8192 | bytes 65536 | tf_op jit(solution)/shard_map/psum | solution.py:59
  119.7 1.4 fusion.6
  121.1 0.7 scatter_custom_fusion.2
  121.9 4.4 %all-gather.6 = f32[2,1,3072]{2,1,0:T(1,128)S(1)} all-gather(f32[1,1,3072]{2,1,0:T(1,128)S(1)} %bitcast.127), channel_id=1, replica_groups=mesh['col'=16,'row'=2] {'row'}, dimensions={0}, use_global_device_ids=true | all-gather | bytes 36864 | tf_op jit(solution)/shard_map/all_gather | solution.py:47
  126.9 2.5 fusion.4
  129.4 0.9 scatter_custom_fusion.3
  130.3 57.6 %psum.64 = f32[8192]{0:T(1024)S(1)} all-reduce(f32[8192]{0:T(1024)S(1)} %bitcast.111), channel_id=1, replica_groups=mesh['col'=16,'row'=2] {'col'}, use_global_device_ids=true, to_apply=%region_7.0 | all-reduce | flops 8192 | bytes 65536 | tf_op jit(solution)/shard_map/psum | solution.py:59
  188.6 1.4 fusion.2
  190.0 0.7 scatter_custom_fusion.4
  190.7 4.4 %all-gather.7 = f32[2,1,3072]{2,1,0:T(1,128)S(1)} all-gather(f32[1,1,3072]{2,1,0:T(1,128)S(1)} %bitcast.128), channel_id=1, replica_groups=mesh['col'=16,'row'=2] {'row'}, dimensions={0}, use_global_device_ids=true | all-gather | bytes 36864 | tf_op jit(solution)/shard_map/all_gather | solution.py:47
  195.2 1.4 fusion.29
  197.1 2.5 fusion
  199.6 0.9 scatter_custom_fusion.5
  200.5 57.6 %psum.65 = f32[8192]{0:T(1024)S(1)} all-reduce(f32[8192]{0:T(1024)S(1)} %bitcast.109), channel_id=1, replica_groups=mesh['col'=16,'row'=2] {'col'}, use_global_device_ids=true, to_apply=%region_11.0 | all-reduce | flops 8192 | bytes 65536 | tf_op jit(solution)/shard_map/psum | solution.py:59
  258.2 1.3 multiply_reduce_fusion.2
  259.4 0.7 multiply_reduce_fusion.4
  260.1 47.5 %all-reduce = (f32[]{:T(128)}, f32[]{:T(128)}, f32[]{:T(128)}, f32[]{:T(128)}, f32[]{:T(128)}, /*index=5*/f32[]{:T(128)}) all-reduce(f32[]{:T(128)} %get-tuple-element.11, f32[]{:T(128)} %get-tuple-element.29, f32[]{:T(128)} %get-tuple-element.10, f32[]{:T(128)} %get-tuple-element.31, ...), channel_id=1, replica_groups=mesh['col'=16,'row'=2] {'col','row'}, use_global_device_ids=true, to_apply=%region_23.0 | all-reduce | flops 6 | bytes 48 | tf_op jit(solution)/shard_map/psum | solution.py:27
  311.9 0.7 copy.13
  (29 shorter events, 3.9 us)
Async XLA Ops:
  0.6 35.7 %copy-start = (f32[1,1,24,128,128]{4,3,2,1,0:T(8,128)S(1)}, f32[1,1,24,128,128]{4,3,2,1,0:T(8,128)}, u32[]{:S(2)}) copy-start(f32[1,1,24,128,128]{4,3,2,1,0:T(8,128)} %param.9) | copy-start | bytes 4718596
  0.6 37.8 %copy-start.2 = (s32[1,1,24]{2,1,0:T(1,128)S(1)}, s32[1,1,24]{2,1,0:T(1,128)}, u32[]{:S(2)}) copy-start(s32[1,1,24]{2,1,0:T(1,128)} %param.11) | copy-start | bytes 292
  0.7 43.0 %copy-start.1 = (f32[512]{0:T(512)S(1)}, f32[512]{0:T(512)}, u32[]{:S(2)}) copy-start(f32[512]{0:T(512)} %param.13) | copy-start | bytes 6148
